TPU v7x, 32 devices: a whole 2x2x4 slice. The times are simulated.
32 devices in a mesh: section: 2 (over core), dp: 8 (over z, x), tensor: 2 (over y).
Axes of the slice: x: 2, y: 2, z: 4, core: 2. Of those that a mesh axis runs over, the one named last changes fastest.
Arguments:
- tokens: bfloat16 [1024, 4096], P('dp', 'tensor'), may hold values from -6 to 6
- gain: bfloat16 [2, 4096], P('section', 'tensor'), may hold values from 0.099609375 to 1.8984375
- w_up: bfloat16 [2, 4096, 5120], P('section', 'dp', 'tensor'), may hold values from -0.09375 to 0.09375
- w_down: bfloat16 [2, 5120, 4096], P('section', 'tensor', 'dp'), may hold values from -0.078125 to 0.078125
- cotangent: bfloat16 [2, 1024, 4096], P('section', 'dp'), may hold values from -6 to 6
Outputs:
- states: bfloat16 [2, 1024, 4096], P('section', 'dp', 'tensor')
- grad_down: bfloat16 [2, 5120, 4096], P('section', 'tensor', 'dp')
All inputs are finite; a program needn't handle non-finite values.
Results may differ from a plain program's by a relative error of at most 0.02.
Values may be sent and summed in bfloat16 or wider, within the bound.
A program may use at most 128 MiB of HBM per device.

v0:
```python
import jax
import jax.numpy as jnp
from jax import lax
from jax.sharding import PartitionSpec as P

EPS = 1e-06
F32 = jnp.float32
BF16 = jnp.bfloat16


def body(tokens, gain, w_up, w_down, cotangent):
    core = lax.axis_index("section")
    layers = lax.axis_size("section")
    assert layers == 2
    dp_id = lax.axis_index("dp")
    dp_count = lax.axis_size("dp")
    tensor_id = lax.axis_index("tensor")
    tensor_count = lax.axis_size("tensor")
    rows, own_width = tokens.shape
    width = own_width * tensor_count
    slice_width = width // dp_count
    hidden_width = w_up.shape[2]
    half = hidden_width // layers
    other = 1 - core
    all_rows = rows * dp_count

    def swap(array):
        return lax.ppermute(array, "section", [(0, 1), (1, 0)])

    def both(own, got):
        return (jnp.where(core == 0, own, got), jnp.where(core == 0, got, own))

    cot_mine = lax.all_to_all(cotangent[0], "dp", split_axis=1, concat_axis=0, tiled=True)
    half_rows = rows // layers
    tok_half = lax.dynamic_slice_in_dim(tokens, core * half_rows, half_rows, 0)
    tok_full = lax.all_gather(tok_half, "tensor", axis=1, tiled=True)
    tok_f = tok_full.astype(F32)
    sums_half = jnp.sum(tok_f * tok_f, axis=1)
    sums_a, sums_b = both(sums_half, swap(sums_half))
    sums = jnp.concatenate([sums_a, sums_b])
    x_half = lax.all_to_all(tok_full, "dp", split_axis=1, concat_axis=0, tiled=True)
    x_a, x_b = both(x_half, swap(x_half))
    x = jnp.concatenate(
        [
            x_a.reshape(dp_count, half_rows, slice_width),
            x_b.reshape(dp_count, half_rows, slice_width),
        ],
        axis=1,
    ).reshape(all_rows, slice_width)
    gain_all = lax.all_gather(gain, "tensor", axis=1, tiled=True)
    gain_own = lax.dynamic_slice_in_dim(gain_all, dp_id * slice_width, slice_width, 1)
    gains = both(gain_own, swap(gain_own))
    up_parts = both(
        lax.dynamic_slice_in_dim(w_up[0], core * half, half, 1),
        swap(lax.dynamic_slice_in_dim(w_up[0], other * half, half, 1)),
    )
    down_parts = both(
        lax.dynamic_slice_in_dim(w_down[0], core * half, half, 0),
        swap(lax.dynamic_slice_in_dim(w_down[0], other * half, half, 0)),
    )
    states = []
    hiddens = []
    for layer in range(layers):
        x_f = x.astype(F32)
        if layer > 0:
            sums = lax.psum_scatter(
                jnp.sum(x_f * x_f, axis=1), "dp", scatter_dimension=0, tiled=True
            )
        scaled = (x_f * gains[layer].astype(F32)).astype(BF16)
        part = jnp.dot(scaled, up_parts[layer], preferred_element_type=F32).astype(BF16)
        pre = lax.psum_scatter(part, "dp", scatter_dimension=0, tiled=True)
        inverse_rms = lax.rsqrt(sums / width + EPS)
        hidden = jax.nn.gelu(pre.astype(F32) * inverse_rms[:, None], approximate=True).astype(BF16)
        hidden_all = lax.all_gather(hidden, "dp", axis=0, tiled=True)
        hiddens.append(hidden_all)
        out = jnp.dot(hidden_all, down_parts[layer], preferred_element_type=F32)
        mid = all_rows // layers
        keep = lax.dynamic_slice_in_dim(out, core * mid, mid, 0)
        give = lax.dynamic_slice_in_dim(out, other * mid, mid, 0).astype(BF16)
        summed = keep + swap(give).astype(F32)
        if tensor_count == 2:
            sent = summed.astype(BF16)
            got = lax.ppermute(sent, "tensor", [(0, 1), (1, 0)])
            summed = sent.astype(F32) + got.astype(F32)
        else:
            summed = lax.psum(summed.astype(BF16), "tensor").astype(F32)
        x_mid = lax.dynamic_slice_in_dim(x_f, core * mid, mid, 0)
        new_mid = (x_mid + summed).astype(BF16)
        new_a, new_b = both(new_mid, swap(new_mid))
        x = jnp.concatenate([new_a, new_b], axis=0)
        states.append(x)
    state_own = jnp.where(core == 0, states[0], states[1])
    state_rows = lax.all_to_all(state_own, "dp", split_axis=0, concat_axis=1, tiled=True)
    state = lax.dynamic_slice_in_dim(state_rows, tensor_id * own_width, own_width, 1)
    hid_keep = jnp.where(core == 0, hiddens[0], hiddens[1])
    hid_got = swap(jnp.where(core == 0, hiddens[1], hiddens[0]))
    hid_parts = both(hid_keep, hid_got)
    hidden_whole = jnp.concatenate(hid_parts, axis=1)
    grad = lax.dot_general(
        hidden_whole, cot_mine, (((0,), (0,)), ((), ())), preferred_element_type=F32
    ).astype(BF16)
    return (state[None], grad[None])


def solution(mesh):
    placed = (
        P("dp", "tensor"),
        P("section", "tensor"),
        P("section", "dp", "tensor"),
        P("section", "tensor", "dp"),
        P("section", "dp", None),
    )
    return jax.shard_map(
        body,
        mesh=mesh,
        in_specs=placed,
        out_specs=(P("section", "dp", "tensor"), P("section", "tensor", "dp")),
        check_vma=False,
    )
```

profile of v0, /device:TPU:0, one launch (start us, length us, event | category | flops | bytes accessed | tf_op | source)
XLA Modules:
  0.0 413.5 jit_solution(5616129061812105178)
XLA Ops:
  7.2 1.0 copy-done
  8.2 10.0 %all_gather.12 = bf16[64,4096]{1,0:T(8,128)(2,1)S(1)} all-gather(bf16[64,2048]{1,0:T(8,128)(2,1)S(1)} %constant_dynamic-slice_fusion.2), channel_id=1, replica_groups=mesh['section'=2,'dp'=8,'tensor'=2] {'tensor'}, dimensions={1}, use_global_device_ids=true | all-gather | bytes 786432 | tf_op jit(solution)/shard_map/all_gather | solution.py:36
  18.2 0.8 copy.22
  19.0 6.2 %all-to-all-start = ((bf16[64,8,512]{2,0,1:T(8,128)(2,1)}), bf16[64,8,512]{2,0,1:T(8,128)(2,1)S(1)}, u32[]{:S(2)}, u32[]{:S(2)}) async-start(bf16[64,8,512]{2,0,1:T(8,128)(2,1)} %bitcast.43), calls=%async_computation | async-start | bytes 1048576 | tf_op jit(solution)/shard_map/all_to_all | solution.py:41
  25.3 2.5 dynamic-slice_bitcast_fusion.1
  27.7 11.2 %all-to-all-done = bf16[64,8,512]{2,0,1:T(8,128)(2,1)S(1)} async-done(((bf16[64,8,512]{2,0,1:T(8,128)(2,1)}), bf16[64,8,512]{2,0,1:T(8,128)(2,1)S(1)}, u32[]{:S(2)}, u32[]{:S(2)}) %all-to-all-start) | async-done | bytes 524320 | tf_op jit(solution)/shard_map/all_to_all | solution.py:41
  38.9 4.3 %all_gather.13 = bf16[1,4096]{1,0:T(2,128)(2,1)S(1)} all-gather(bf16[1,2048]{1,0:T(2,128)(2,1)S(1)} %copy-done.12), channel_id=1, replica_groups=mesh['section'=2,'dp'=8,'tensor'=2] {'tensor'}, dimensions={1}, use_global_device_ids=true | all-gather | bytes 12288 | tf_op jit(solution)/shard_map/all_gather | solution.py:50
  43.3 1.1 collective-permute-done.1
  44.4 0.1 broadcast_select_fusion.9
  44.7 0.3 bitcast_convert_fusion
  45.0 1.4 copy-done.10
  46.4 3.1 convolution_convert_fusion.1
  49.5 0.2 multiply_reduce_fusion.1
  49.7 1.5 collective-permute-start.3
  51.3 0.8 collective-permute-done.3
  52.1 0.1 fusion.48
  52.2 68.8 %reduce-scatter.3.cloned.1.call-done = bf16[128,1280]{1,0:T(8,128)(2,1)} async-done(((bf16[1024,1280]{1,0:T(8,128)(2,1)}), bf16[128,1280]{1,0:T(8,128)(2,1)}) %reduce-scatter.3.cloned.1.call-update) | async-done | bytes 327696 | tf_op jit(solution)/shard_map/reduce_scatter | solution.py:71
  120.9 2.0 fusion.30
  123.0 2.5 dynamic-slice_bitcast_fusion
  125.5 3.4 collective-permute-done.4
  128.9 48.4 %all-gather.3.cloned.1.call-done = bf16[1024,1280]{1,0:T(8,128)(2,1)} async-done(((bf16[128,1280]{1,0:T(8,128)(2,1)}), bf16[1024,1280]{1,0:T(8,128)(2,1)}) %all-gather.3.cloned.1.call-update) | async-done | bytes 2621456 | tf_op jit(solution)/shard_map/all_gather | solution.py:74
  177.3 3.7 fusion.10
  181.0 1.3 copy-done.8
  182.3 0.9 dynamic-slice_convert_fusion.1
  183.1 2.1 collective-permute-done.5
  185.3 1.4 add_convert_fusion.3
  186.7 1.5 collective-permute-start.6
  188.2 12.5 %collective-permute-done.6 = bf16[512,512]{1,0:T(8,128)(2,1)S(1)} collective-permute-done((bf16[512,512]{1,0:T(8,128)(2,1)S(1)}, bf16[512,512]{1,0:T(8,128)(2,1)S(1)}, u32[]{:S(2)}, u32[]{:S(2)}) %collective-permute-start.6) | collective-permute-done | bytes 524320 | tf_op jit(solution)/shard_map/ppermute | solution.py:83
  200.7 0.2 add_convert_fusion.2
  201.0 1.9 collective-permute-done.7
  202.9 0.1 broadcast_select_fusion.7
  203.0 4.8 %convolution_convert_fusion = bf16[1024,1280]{1,0:T(8,128)(2,1)} fusion(bf16[512,1280]{1,0:T(8,128)(2,1)} %collective-permute-done.2, pred[]{:T(512)S(6)} %eq.2, bf16[1,512,2560]{2,1,0:T(8,128)(2,1)S(1)} %copy-done.11, s32[]{:T(128)S(6)} %select_n.145, f32[512]{0:T(512)S(1)} %bitcast.52, bf16[512,512]{1,0:T(8,128)(2,1)S(1)} %get-tuple-element.7, ...), kind=kOutput, calls=%fused_computation.6 | convolution fusion | flops 1347289088 | bytes 6293509 | tf_op jit(solution)/shard_map/dot_general | solution.py:70
  207.8 0.6 copy-done.13
  208.4 0.6 dynamic-slice.4
  209.7 0.3 multiply_reduce_fusion
  209.9 19.5 %all-reduce = f32[1024]{0:T(1024)S(1)} all-reduce(f32[1024]{0:T(1024)S(1)} %multiply_reduce_fusion), channel_id=4, replica_groups=mesh['section'=2,'dp'=8,'tensor'=2] {'dp'}, use_global_device_ids=true, to_apply=%region_4.5.clone | all-reduce | flops 1024 | bytes 8192
  229.5 0.1 fusion.47
  229.5 48.0 %reduce-scatter.5.cloned.1.call-done = bf16[128,1280]{1,0:T(8,128)(2,1)} async-done(((bf16[1024,1280]{1,0:T(8,128)(2,1)}), bf16[128,1280]{1,0:T(8,128)(2,1)}) %reduce-scatter.5.cloned.1.call-update) | async-done | bytes 327696 | tf_op jit(solution)/shard_map/reduce_scatter | solution.py:71
  277.5 2.0 fusion.38
  279.5 54.1 %all-gather.5.cloned.1.call-done = bf16[1024,1280]{1,0:T(8,128)(2,1)} async-done(((bf16[128,1280]{1,0:T(8,128)(2,1)}), bf16[1024,1280]{1,0:T(8,128)(2,1)}) %all-gather.5.cloned.1.call-update) | async-done | bytes 2621456 | tf_op jit(solution)/shard_map/all_gather | solution.py:74
  333.7 4.2 %fusion.11 = f32[1024,512]{1,0:T(8,128)S(1)} fusion(bf16[1024,1280]{1,0:T(8,128)(2,1)} %all-gather.5.cloned.1.call-done, bf16[1280,512]{1,0:T(8,128)(2,1)} %collective-permute-done.4, pred[]{:T(512)S(6)} %eq.2, bf16[1,2560,512]{2,1,0:T(8,128)(2,1)} %param.8, s32[]{:T(128)S(6)} %select_n.145), kind=kOutput, calls=%fused_computation.18 | convolution fusion | flops 1342832640 | bytes 7340037 | tf_op jit(solution)/shard_map/dot_general | solution.py:76
  337.9 1.3 copy-done.7
  339.2 0.9 dynamic-slice_convert_fusion
  340.0 1.8 broadcast_select_fusion.2
  341.9 0.5 collective-permute-start.11
  342.4 2.3 copy.18
  344.7 4.2 %all-to-all-start.2 = ((bf16[128,8,512]{0,2,1:T(8,128)(2,1)}), bf16[128,8,512]{0,2,1:T(8,128)(2,1)}, u32[]{:S(2)}, u32[]{:S(2)}) async-start(bf16[128,8,512]{0,2,1:T(8,128)(2,1)} %bitcast.45), calls=%async_computation.4 | async-start | bytes 2097152 | tf_op jit(solution)/shard_map/all_to_all | solution.py:33
  348.9 1.6 add_convert_fusion.1
  350.6 1.5 collective-permute-start.9
  352.1 0.3 fusion.50
  352.4 12.1 %collective-permute-done.9 = bf16[512,512]{1,0:T(8,128)(2,1)S(1)} collective-permute-done((bf16[512,512]{1,0:T(8,128)(2,1)S(1)}, bf16[512,512]{1,0:T(8,128)(2,1)S(1)}, u32[]{:S(2)}, u32[]{:S(2)}) %collective-permute-start.9) | collective-permute-done | bytes 524320 | tf_op jit(solution)/shard_map/ppermute | solution.py:83
  364.5 0.2 add_convert_fusion
  364.8 1.9 collective-permute-done.10
  366.7 0.1 broadcast_select_fusion.5
  366.8 1.2 maximum_select_fusion
  368.0 2.3 copy.16
  370.3 4.8 %all-to-all-done.2 = bf16[128,8,512]{0,2,1:T(8,128)(2,1)} async-done(((bf16[128,8,512]{0,2,1:T(8,128)(2,1)}), bf16[128,8,512]{0,2,1:T(8,128)(2,1)}, u32[]{:S(2)}, u32[]{:S(2)}) %all-to-all-start.2) | async-done | bytes 1048608 | tf_op jit(solution)/shard_map/all_to_all | solution.py:33
  375.1 4.4 %all-to-all-start.1 = ((bf16[8,128,512]{1,2,0:T(8,128)(2,1)}), bf16[8,128,512]{1,2,0:T(8,128)(2,1)}, u32[]{:S(2)}, u32[]{:S(2)}) async-start(bf16[8,128,512]{1,2,0:T(8,128)(2,1)} %copy.16), calls=%async_computation.3 | async-start | bytes 2097152 | tf_op jit(solution)/shard_map/all_to_all | solution.py:93
  379.6 2.3 copy.19
  381.8 2.3 broadcast_select_fusion.1
  384.1 4.3 %fusion.7 = bf16[1,2560,512]{2,1,0:T(8,128)(2,1)} fusion(bf16[1024,512]{1,0:T(8,128)(2,1)S(1)} %bitcast.50, bf16[1024,1280]{1,0:T(8,128)(2,1)S(1)} %get-tuple-element.3, bf16[1024,1280]{1,0:T(8,128)(2,1)S(1)} %get-tuple-element.2), kind=kOutput, calls=%fused_computation.5 | convolution fusion | flops 2696151040 | bytes 8912896 | tf_op jit(solution)/shard_map/dot_general | solution.py:99
  388.4 16.5 %all-to-all-done.1 = bf16[8,128,512]{1,2,0:T(8,128)(2,1)} async-done(((bf16[8,128,512]{1,2,0:T(8,128)(2,1)}), bf16[8,128,512]{1,2,0:T(8,128)(2,1)}, u32[]{:S(2)}, u32[]{:S(2)}) %all-to-all-start.1) | async-done | bytes 1048608 | tf_op jit(solution)/shard_map/all_to_all | solution.py:93
  404.9 1.1 constant_dynamic-slice_fusion
  405.9 1.0 copy.17
  (48 shorter events, 0.6 us)
Async XLA Ops:
  7.2 1.0 copy-start
  19.0 19.8 %copy-start.12 = (bf16[1,2048]{1,0:T(2,128)(2,1)S(1)}, bf16[1,2048]{1,0:T(2,128)(2,1)}, u32[]{:S(2)}) copy-start(bf16[1,2048]{1,0:T(2,128)(2,1)} %param.6) | copy-start | bytes 12292
  19.0 19.8 %all-to-all-start = ((bf16[64,8,512]{2,0,1:T(8,128)(2,1)}), bf16[64,8,512]{2,0,1:T(8,128)(2,1)S(1)}, u32[]{:S(2)}, u32[]{:S(2)}) async-start(bf16[64,8,512]{2,0,1:T(8,128)(2,1)} %bitcast.43), calls=%async_computation | async-start | bytes 1048576 | tf_op jit(solution)/shard_map/all_to_all | solution.py:41
  25.2 95.7 %reduce-scatter.3.cloned.1.call-start = ((), (), s32[]{:S(2)}) async-start(), calls=%async_computation.5 | async-start | bytes 2949120 | tf_op jit(solution)/shard_map/reduce_scatter | solution.py:71
  27.7 17.3 %collective-permute-start.2 = (bf16[512,1280]{1,0:T(8,128)(2,1)}, bf16[512,1280]{1,0:T(8,128)(2,1)}, u32[]{:S(2)}, u32[]{:S(2)}) collective-permute-start(bf16[512,1280]{1,0:T(8,128)(2,1)} %dynamic-slice_bitcast_fusion.1), channel_id=1, source_target_pairs={{0,16},{16,0},{1,17},{17,1},{2,18},{18,2},{3,19},{19,3},{4,20},{20... | collective-permute-start | bytes 3932168 | tf_op jit(solution)/shard_map/ppermute | solution.py:28
  38.9 5.6 %collective-permute-start = (bf16[512,512]{1,0:T(8,128)(2,1)S(1)}, bf16[512,512]{1,0:T(8,128)(2,1)S(1)}, u32[]{:S(2)}, u32[]{:S(2)}) collective-permute-start(bf16[512,512]{1,0:T(8,128)(2,1)S(1)} %bitcast.47), channel_id=1, source_target_pairs={{0,16},{16,0},{1,17},{17,1},{2,18},{18,2},{3,19},{19,3},{4,20},{20... | collective-permute-start | bytes 1572872 | tf_op jit(solution)/shard_map/ppermute | solution.py:28
  43.2 1.2 collective-permute-start.1
  44.6 1.7 copy-start.10
  49.5 127.8 %all-gather.3.cloned.1.call-start = ((), (), s32[]{:S(2)}) async-start(), calls=%async_computation.6 | async-start | bytes 2949120 | tf_op jit(solution)/shard_map/all_gather | solution.py:74
  49.7 2.3 collective-permute-start.3
  123.0 154.5 %reduce-scatter.5.cloned.1.call-start = ((), (), s32[]{:S(2)}) async-start(), calls=%async_computation.7 | async-start | bytes 2949120 | tf_op jit(solution)/shard_map/reduce_scatter | solution.py:71
  125.5 3.4 collective-permute-start.4
  180.9 1.3 copy-start.8
  183.1 2.1 collective-permute-start.5
  186.6 16.3 %copy-start.11 = (bf16[1,512,2560]{2,1,0:T(8,128)(2,1)S(1)}, bf16[1,512,2560]{2,1,0:T(8,128)(2,1)}, u32[]{:S(2)}) copy-start(bf16[1,512,2560]{2,1,0:T(8,128)(2,1)} %param.7) | copy-start | bytes 7864324
  186.7 14.0 %collective-permute-start.6 = (bf16[512,512]{1,0:T(8,128)(2,1)S(1)}, bf16[512,512]{1,0:T(8,128)(2,1)S(1)}, u32[]{:S(2)}, u32[]{:S(2)}) collective-permute-start(bf16[512,512]{1,0:T(8,128)(2,1)S(1)} %add_convert_fusion.3), channel_id=1, source_target_pairs={{0,1},{1,0},{2,3},{3,2},{4,5},{5,4},{6,7},{7,6},{8,9},{9,8},{10,11... | collective-permute-start | bytes 1572872 | tf_op jit(solution)/shard_map/ppermute | solution.py:83
  200.9 2.0 collective-permute-start.7
  203.0 6.7 %copy-start.3 = (bf16[512,512]{1,0:T(8,128)(2,1)}, bf16[512,512]{1,0:T(8,128)(2,1)S(1)}, u32[]{:S(2)}) copy-start(bf16[512,512]{1,0:T(8,128)(2,1)S(1)} %get-tuple-element.6) | copy-start | bytes 1572868
  203.0 6.7 %copy-start.5 = (bf16[512,512]{1,0:T(8,128)(2,1)}, bf16[512,512]{1,0:T(8,128)(2,1)S(1)}, u32[]{:S(2)}) copy-start(bf16[512,512]{1,0:T(8,128)(2,1)S(1)} %get-tuple-element.7) | copy-start | bytes 1572868
  207.7 0.7 copy-start.13
  207.8 125.9 %all-gather.5.cloned.1.call-start = ((), (), s32[]{:S(2)}) async-start(), calls=%async_computation.8 | async-start | bytes 2949120 | tf_op jit(solution)/shard_map/all_gather | solution.py:74
  333.6 6.4 %copy-start.1 = (bf16[1024,1280]{1,0:T(8,128)(2,1)S(1)}, bf16[1024,1280]{1,0:T(8,128)(2,1)}, u32[]{:S(2)}) copy-start(bf16[1024,1280]{1,0:T(8,128)(2,1)} %all-gather.3.cloned.1.call-done) | copy-start | bytes 7864324
  333.6 6.4 %copy-start.2 = (bf16[1024,1280]{1,0:T(8,128)(2,1)S(1)}, bf16[1024,1280]{1,0:T(8,128)(2,1)}, u32[]{:S(2)}) copy-start(bf16[1024,1280]{1,0:T(8,128)(2,1)} %all-gather.5.cloned.1.call-done) | copy-start | bytes 7864324
  337.8 1.3 copy-start.7
  340.0 8.9 %collective-permute-start.8 = (bf16[512,512]{1,0:T(8,128)(2,1)}, bf16[512,512]{1,0:T(8,128)(2,1)}, u32[]{:S(2)}, u32[]{:S(2)}) collective-permute-start(bf16[512,512]{1,0:T(8,128)(2,1)} %dynamic-slice_convert_fusion), channel_id=1, source_target_pairs={{0,16},{16,0},{1,17},{17,1},{2,18},{18,2},{3,19},{19,3},{4,20},{20... | collective-permute-start | bytes 1572872 | tf_op jit(solution)/shard_map/ppermute | solution.py:28
  341.9 40.0 %collective-permute-start.11 = (bf16[1024,1280]{1,0:T(8,128)(2,1)}, bf16[1024,1280]{1,0:T(8,128)(2,1)}, u32[]{:S(2)}, u32[]{:S(2)}) collective-permute-start(bf16[1024,1280]{1,0:T(8,128)(2,1)} %broadcast_select_fusion.2), channel_id=1, source_target_pairs={{0,16},{16,0},{1,17},{17,1},{2,18},{18,2},{3,19},{19,3},{4,20},{20... | collective-permute-start | bytes 7864328 | tf_op jit(solution)/shard_map/ppermute | solution.py:28
  344.7 30.5 %all-to-all-start.2 = ((bf16[128,8,512]{0,2,1:T(8,128)(2,1)}), bf16[128,8,512]{0,2,1:T(8,128)(2,1)}, u32[]{:S(2)}, u32[]{:S(2)}) async-start(bf16[128,8,512]{0,2,1:T(8,128)(2,1)} %bitcast.45), calls=%async_computation.4 | async-start | bytes 2097152 | tf_op jit(solution)/shard_map/all_to_all | solution.py:33
  348.9 3.2 copy-start.4
  348.9 3.2 copy-start.6
  350.6 13.9 %collective-permute-start.9 = (bf16[512,512]{1,0:T(8,128)(2,1)S(1)}, bf16[512,512]{1,0:T(8,128)(2,1)S(1)}, u32[]{:S(2)}, u32[]{:S(2)}) collective-permute-start(bf16[512,512]{1,0:T(8,128)(2,1)S(1)} %add_convert_fusion.1), channel_id=1, source_target_pairs={{0,1},{1,0},{2,3},{3,2},{4,5},{5,4},{6,7},{7,6},{8,9},{9,8},{10,11... | collective-permute-start | bytes 1572872 | tf_op jit(solution)/shard_map/ppermute | solution.py:83
  364.7 2.0 collective-permute-start.10
  375.1 29.8 %all-to-all-start.1 = ((bf16[8,128,512]{1,2,0:T(8,128)(2,1)}), bf16[8,128,512]{1,2,0:T(8,128)(2,1)}, u32[]{:S(2)}, u32[]{:S(2)}) async-start(bf16[8,128,512]{1,2,0:T(8,128)(2,1)} %copy.16), calls=%async_computation.3 | async-start | bytes 2097152 | tf_op jit(solution)/shard_map/all_to_all | solution.py:93
  381.8 2.3 copy-start.9
Sparse Core Ops, SparseCore 0:
  49.6 71.2 reduce-scatter.2
  123.7 53.5 all-gather.2
  207.9 69.5 reduce-scatter.4
  280.1 53.4 all-gather.4
where the time goes:
time: 414 us; the launch traced here: 413 us
  waiting for transfers between devices  288 us (70%)
  blocking collectives  33.8 us (8%)
  local copies, waits for them, and re-layouts  22.6 us (5%)
  starting transfers between devices  20.3 us (5%)
  matrix products  20 us (5%)
  between operations  14.7 us (4%)
  other arithmetic  14.5 us (4%)
    reduce_scatter x2, waiting for transfers between devices, body(): pre = lax.psum_scatter(part, 'dp', scatter_dimension=0, tiled=True)  117 us
    all_gather x2, waiting for transfers between devices, body(): hidden_all = lax.all_gather(hidden, 'dp', axis=0, tiled=True)  103 us
    ppermute x2, waiting for transfers between devices, body(): got = lax.ppermute(sent, 'tensor', [(0, 1), (1, 0)])  24.6 us
    unnamed x1, blocking collectives  19.5 us
    all_to_all x1, waiting for transfers between devices, body(): lax.all_to_all(state_own, 'dp', split_axis=0, concat_axis=1, tiled=True)  16.5 us
    ppermute x10, waiting for transfers between devices, swap(): return lax.ppermute(array, 'section', [(0, 1), (1, 0)])  11.3 us
    all_to_all x1, waiting for transfers between devices, body(): lax.all_to_all(tok_full, 'dp', split_axis=1, concat_axis=0, tiled=True)  11.2 us
    all_gather x1, blocking collectives, body(): tok_full = lax.all_gather(tok_half, 'tensor', axis=1, tiled=True)  9.97 us
  transfers between devices with their start and end apart: 19, of which 15 were waited for; matrix products, arithmetic and copies ran while one was open for 6% of the time, Pallas kernels for 0%

commit v1 on v0

--- a/solution.py
+++ b/solution.py
@@ -6,6 +6,16 @@
 EPS = 1e-06
 F32 = jnp.float32
 BF16 = jnp.bfloat16
+
+
+def turned_line(x, axis, d):
+    size = lax.axis_size(axis)
+    held, blocks = (x, [x])
+    for _ in range(size - 1):
+        held = lax.ppermute(held, axis, [(i, (i + 1) % size) for i in range(size)])
+        blocks.insert(0, held)
+    flat = jnp.concatenate(blocks, axis=d)
+    return jnp.roll(flat, (lax.axis_index(axis) + 1) * x.shape[d], axis=d)
 
 
 def body(tokens, gain, w_up, w_down, cotangent):
@@ -71,7 +81,7 @@
         pre = lax.psum_scatter(part, "dp", scatter_dimension=0, tiled=True)
         inverse_rms = lax.rsqrt(sums / width + EPS)
         hidden = jax.nn.gelu(pre.astype(F32) * inverse_rms[:, None], approximate=True).astype(BF16)
-        hidden_all = lax.all_gather(hidden, "dp", axis=0, tiled=True)
+        hidden_all = turned_line(hidden, "dp", 0)
         hiddens.append(hidden_all)
         out = jnp.dot(hidden_all, down_parts[layer], preferred_element_type=F32)
         mid = all_rows // layers

time: 414 us -> 460 us (1.11)
  waiting for transfers between devices: 288 us -> 322 us
  other arithmetic: 14.5 us -> 22.2 us
  local copies, waits for them, and re-layouts: 22.6 us -> 27.8 us
    ppermute x0 -> x14, waiting for transfers between devices: none -> 144 us  [turned_line(): held = lax.ppermute(held, axis, [(i, (i + 1) % size) for i in range(size)])]
    all_gather x2 -> x0, waiting for transfers between devices: 103 us -> none  [body(): hidden_all = lax.all_gather(hidden, 'dp', axis=0, tiled=True)]
    unnamed x30 -> x64, local copies, waits for them, and re-layouts: 8.5 us -> 16.7 us
  transfers between devices with their start and end apart: 19 -> 31, of which waited for: 15 -> 26; matrix products, arithmetic and copies ran while one was open for 6% -> 7% of each run, Pallas kernels for 0% -> 0%
where the time goes in v1:
time: 460 us; the launch traced here: 459 us
  waiting for transfers between devices  322 us (70%)
  blocking collectives  31.9 us (7%)
  local copies, waits for them, and re-layouts  27.8 us (6%)
  other arithmetic  22.2 us (5%)
  starting transfers between devices  21.8 us (5%)
  matrix products  17.9 us (4%)
  between operations  15.2 us (3%)
    ppermute x14, waiting for transfers between devices, turned_line(): held = lax.ppermute(held, axis, [(i, (i + 1) % size) for i in range(size)])  144 us
    reduce_scatter x2, waiting for transfers between devices, body(): pre = lax.psum_scatter(part, 'dp', scatter_dimension=0, tiled=True)  116 us
    ppermute x2, waiting for transfers between devices, body(): got = lax.ppermute(sent, 'tensor', [(0, 1), (1, 0)])  23.5 us
    unnamed x1, blocking collectives  17.6 us
    unnamed x64, local copies, waits for them, and re-layouts  16.7 us
    all_to_all x1, waiting for transfers between devices, body(): lax.all_to_all(state_own, 'dp', split_axis=0, concat_axis=1, tiled=True)  13.4 us
    all_to_all x1, waiting for transfers between devices, body(): lax.all_to_all(tok_full, 'dp', split_axis=1, concat_axis=0, tiled=True)  12.1 us
    all_gather x1, blocking collectives, body(): tok_full = lax.all_gather(tok_half, 'tensor', axis=1, tiled=True)  9.97 us
  transfers between devices with their start and end apart: 31, of which 26 were waited for; matrix products, arithmetic and copies ran while one was open for 7% of the time, Pallas kernels for 0%

profile of v1, /device:TPU:0, one launch (start us, length us, event | category | flops | bytes accessed | tf_op | source)
XLA Modules:
  0.0 458.7 jit_solution(12929232081435340537)
XLA Ops:
  7.2 1.0 copy-done
  8.2 10.0 %all_gather.6 = bf16[64,4096]{1,0:T(8,128)(2,1)S(1)} all-gather(bf16[64,2048]{1,0:T(8,128)(2,1)S(1)} %constant_dynamic-slice_fusion.2), channel_id=1, replica_groups=mesh['section'=2,'dp'=8,'tensor'=2] {'tensor'}, dimensions={1}, use_global_device_ids=true | all-gather | bytes 786432 | tf_op jit(solution)/shard_map/all_gather | solution.py:46
  19.1 6.0 %all-to-all-start = ((bf16[64,8,512]{2,0,1:T(8,128)(2,1)}), bf16[64,8,512]{2,0,1:T(8,128)(2,1)S(1)}, u32[]{:S(2)}, u32[]{:S(2)}) async-start(bf16[64,8,512]{2,0,1:T(8,128)(2,1)} %bitcast.43), calls=%async_computation | async-start | bytes 1048576 | tf_op jit(solution)/shard_map/all_to_all | solution.py:51
  25.1 1.4 dynamic-slice_bitcast_fusion.1
  26.6 12.1 %all-to-all-done = bf16[64,8,512]{2,0,1:T(8,128)(2,1)S(1)} async-done(((bf16[64,8,512]{2,0,1:T(8,128)(2,1)}), bf16[64,8,512]{2,0,1:T(8,128)(2,1)S(1)}, u32[]{:S(2)}, u32[]{:S(2)}) %all-to-all-start) | async-done | bytes 524320 | tf_op jit(solution)/shard_map/all_to_all | solution.py:51
  38.8 4.3 all_gather.7
  43.2 1.1 collective-permute-done.1
  44.9 1.3 copy-done.5
  46.9 3.1 convolution_convert_fusion.1
  50.3 1.5 collective-permute-start.3
  52.7 68.6 %reduce-scatter.3.cloned.1.call-done = bf16[128,1280]{1,0:T(8,128)(2,1)} async-done(((bf16[1024,1280]{1,0:T(8,128)(2,1)}), bf16[128,1280]{1,0:T(8,128)(2,1)}) %reduce-scatter.3.cloned.1.call-update) | async-done | bytes 327696 | tf_op jit(solution)/shard_map/reduce_scatter | solution.py:81
  121.3 1.3 fusion.32
  123.5 10.0 %collective-permute-done.4 = bf16[128,1280]{1,0:T(8,128)(2,1)S(1)} collective-permute-done((bf16[128,1280]{1,0:T(8,128)(2,1)S(1)}, bf16[128,1280]{1,0:T(8,128)(2,1)S(1)}, u32[]{:S(2)}, u32[]{:S(2)}) %collective-permute-start.4) | collective-permute-done | bytes 327712 | tf_op jit(solution)/shard_map/ppermute | solution.py:15
  133.4 9.9 %collective-permute-done.5 = bf16[128,1280]{1,0:T(8,128)(2,1)S(1)} collective-permute-done((bf16[128,1280]{1,0:T(8,128)(2,1)S(1)}, bf16[128,1280]{1,0:T(8,128)(2,1)S(1)}, u32[]{:S(2)}, u32[]{:S(2)}) %collective-permute-start.5) | collective-permute-done | bytes 327712 | tf_op jit(solution)/shard_map/ppermute | solution.py:15
  143.4 9.8 %collective-permute-done.6 = bf16[128,1280]{1,0:T(8,128)(2,1)S(1)} collective-permute-done((bf16[128,1280]{1,0:T(8,128)(2,1)S(1)}, bf16[128,1280]{1,0:T(8,128)(2,1)S(1)}, u32[]{:S(2)}, u32[]{:S(2)}) %collective-permute-start.6) | collective-permute-done | bytes 327712 | tf_op jit(solution)/shard_map/ppermute | solution.py:15
  153.9 9.8 %collective-permute-done.7 = bf16[128,1280]{1,0:T(8,128)(2,1)S(1)} collective-permute-done((bf16[128,1280]{1,0:T(8,128)(2,1)S(1)}, bf16[128,1280]{1,0:T(8,128)(2,1)S(1)}, u32[]{:S(2)}, u32[]{:S(2)}) %collective-permute-start.7) | collective-permute-done | bytes 327712 | tf_op jit(solution)/shard_map/ppermute | solution.py:15
  164.4 10.4 %collective-permute-done.8 = bf16[128,1280]{1,0:T(8,128)(2,1)S(1)} collective-permute-done((bf16[128,1280]{1,0:T(8,128)(2,1)S(1)}, bf16[128,1280]{1,0:T(8,128)(2,1)S(1)}, u32[]{:S(2)}, u32[]{:S(2)}) %collective-permute-start.8) | collective-permute-done | bytes 327712 | tf_op jit(solution)/shard_map/ppermute | solution.py:15
  175.6 12.1 %collective-permute-done.9 = bf16[128,1280]{1,0:T(8,128)(2,1)} collective-permute-done((bf16[128,1280]{1,0:T(8,128)(2,1)S(1)}, bf16[128,1280]{1,0:T(8,128)(2,1)}, u32[]{:S(2)}, u32[]{:S(2)}) %collective-permute-start.9) | collective-permute-done | bytes 327712 | tf_op jit(solution)/shard_map/ppermute | solution.py:15
  187.7 1.1 dynamic-slice_bitcast_fusion
  188.8 8.9 %collective-permute-done.10 = bf16[128,1280]{1,0:T(8,128)(2,1)} collective-permute-done((bf16[128,1280]{1,0:T(8,128)(2,1)}, bf16[128,1280]{1,0:T(8,128)(2,1)}, u32[]{:S(2)}, u32[]{:S(2)}) %collective-permute-start.10) | collective-permute-done | bytes 327712 | tf_op jit(solution)/shard_map/ppermute | solution.py:15
  197.8 1.0 constant_dynamic-update-slice_fusion.7
  198.7 1.0 constant_dynamic-update-slice_fusion.6
  199.7 1.0 constant_dynamic-update-slice_fusion.5
  200.7 1.0 constant_dynamic-update-slice_fusion.4
  201.7 1.0 constant_dynamic-update-slice_fusion.3
  203.2 2.3 fusion.12
  205.5 1.3 copy-done.10
  207.0 2.0 collective-permute-done.12
  209.0 1.6 add_convert_fusion.3
  210.5 1.5 collective-permute-start.13
  212.1 12.5 %collective-permute-done.13 = bf16[512,512]{1,0:T(8,128)(2,1)S(1)} collective-permute-done((bf16[512,512]{1,0:T(8,128)(2,1)S(1)}, bf16[512,512]{1,0:T(8,128)(2,1)S(1)}, u32[]{:S(2)}, u32[]{:S(2)}) %collective-permute-start.13) | collective-permute-done | bytes 524320 | tf_op jit(solution)/shard_map/ppermute | solution.py:93
  224.9 1.9 collective-permute-done.14
  227.6 4.4 convolution_convert_fusion
  234.0 1.3 multiply_reduce_fusion
  235.3 17.6 %all-reduce = f32[1024]{0:T(1024)S(1)} all-reduce(f32[1024]{0:T(1024)S(1)} %multiply_reduce_fusion), channel_id=4, replica_groups=mesh['section'=2,'dp'=8,'tensor'=2] {'dp'}, use_global_device_ids=true, to_apply=%region_4.6.clone | all-reduce | flops 1024 | bytes 8192
  252.9 47.8 %reduce-scatter.5.cloned.1.call-done = bf16[128,1280]{1,0:T(8,128)(2,1)} async-done(((bf16[1024,1280]{1,0:T(8,128)(2,1)}), bf16[128,1280]{1,0:T(8,128)(2,1)}) %reduce-scatter.5.cloned.1.call-update) | async-done | bytes 327696 | tf_op jit(solution)/shard_map/reduce_scatter | solution.py:81
  300.7 1.4 fusion.40
  302.9 10.0 %collective-permute-done.15 = bf16[128,1280]{1,0:T(8,128)(2,1)S(1)} collective-permute-done((bf16[128,1280]{1,0:T(8,128)(2,1)S(1)}, bf16[128,1280]{1,0:T(8,128)(2,1)S(1)}, u32[]{:S(2)}, u32[]{:S(2)}) %collective-permute-start.15) | collective-permute-done | bytes 327712 | tf_op jit(solution)/shard_map/ppermute | solution.py:15
  312.8 9.9 %collective-permute-done.16 = bf16[128,1280]{1,0:T(8,128)(2,1)S(1)} collective-permute-done((bf16[128,1280]{1,0:T(8,128)(2,1)S(1)}, bf16[128,1280]{1,0:T(8,128)(2,1)S(1)}, u32[]{:S(2)}, u32[]{:S(2)}) %collective-permute-start.16) | collective-permute-done | bytes 327712 | tf_op jit(solution)/shard_map/ppermute | solution.py:15
  322.7 9.8 %collective-permute-done.17 = bf16[128,1280]{1,0:T(8,128)(2,1)S(1)} collective-permute-done((bf16[128,1280]{1,0:T(8,128)(2,1)S(1)}, bf16[128,1280]{1,0:T(8,128)(2,1)S(1)}, u32[]{:S(2)}, u32[]{:S(2)}) %collective-permute-start.17) | collective-permute-done | bytes 327712 | tf_op jit(solution)/shard_map/ppermute | solution.py:15
  332.5 10.1 %collective-permute-done.18 = bf16[128,1280]{1,0:T(8,128)(2,1)S(1)} collective-permute-done((bf16[128,1280]{1,0:T(8,128)(2,1)S(1)}, bf16[128,1280]{1,0:T(8,128)(2,1)S(1)}, u32[]{:S(2)}, u32[]{:S(2)}) %collective-permute-start.18) | collective-permute-done | bytes 327712 | tf_op jit(solution)/shard_map/ppermute | solution.py:15
  342.6 11.2 %collective-permute-done.19 = bf16[128,1280]{1,0:T(8,128)(2,1)S(1)} collective-permute-done((bf16[128,1280]{1,0:T(8,128)(2,1)S(1)}, bf16[128,1280]{1,0:T(8,128)(2,1)S(1)}, u32[]{:S(2)}, u32[]{:S(2)}) %collective-permute-start.19) | collective-permute-done | bytes 327712 | tf_op jit(solution)/shard_map/ppermute | solution.py:15
  353.8 12.4 %collective-permute-done.20 = bf16[128,1280]{1,0:T(8,128)(2,1)S(1)} collective-permute-done((bf16[128,1280]{1,0:T(8,128)(2,1)S(1)}, bf16[128,1280]{1,0:T(8,128)(2,1)S(1)}, u32[]{:S(2)}, u32[]{:S(2)}) %collective-permute-start.20) | collective-permute-done | bytes 327712 | tf_op jit(solution)/shard_map/ppermute | solution.py:15
  366.1 9.8 %collective-permute-done.21 = bf16[128,1280]{1,0:T(8,128)(2,1)S(1)} collective-permute-done((bf16[128,1280]{1,0:T(8,128)(2,1)S(1)}, bf16[128,1280]{1,0:T(8,128)(2,1)S(1)}, u32[]{:S(2)}, u32[]{:S(2)}) %collective-permute-start.21) | collective-permute-done | bytes 327712 | tf_op jit(solution)/shard_map/ppermute | solution.py:15
  376.4 4.9 %broadcast_select_fusion.2 = (bf16[1024,1280]{1,0:T(8,128)(2,1)}, bf16[1024,1280]{1,0:T(8,128)(2,1)S(1)}) fusion(pred[]{:T(512)S(6)} %eq.3, s32[]{:T(128)S(6)} %select_n.182, bf16[1024,1280]{1,0:T(8,128)(2,1)S(1)} %constant_dynamic-update-slice_fusion.8, bf16[1024,1280]{1,0:T(8,128)(2,1)S(1)} %constant_dynamic-update-slice_fusion), kind=kLoop, calls=%fused_computation.16 | loop fusion | flops 11796480 | bytes 10485765 | tf_op jit(solution)/shard_map/jit(_where)/select_n | solution.py:106
  381.3 3.8 fusion.13
  385.2 1.0 dynamic-slice_convert_fusion
  387.2 2.3 copy.18
  389.5 4.3 all-to-all-start.2
  393.7 1.6 add_convert_fusion.1
  395.3 1.5 collective-permute-start.23
  396.8 1.3 fusion.52
  398.2 11.0 %collective-permute-done.23 = bf16[512,512]{1,0:T(8,128)(2,1)S(1)} collective-permute-done((bf16[512,512]{1,0:T(8,128)(2,1)S(1)}, bf16[512,512]{1,0:T(8,128)(2,1)S(1)}, u32[]{:S(2)}, u32[]{:S(2)}) %collective-permute-start.23) | collective-permute-done | bytes 524320 | tf_op jit(solution)/shard_map/ppermute | solution.py:93
  409.5 1.9 collective-permute-done.24
  411.5 1.3 maximum_select_fusion
  412.8 2.3 copy.16
  415.0 4.9 %all-to-all-done.2 = bf16[128,8,512]{0,2,1:T(8,128)(2,1)} async-done(((bf16[128,8,512]{0,2,1:T(8,128)(2,1)}), bf16[128,8,512]{0,2,1:T(8,128)(2,1)}, u32[]{:S(2)}, u32[]{:S(2)}) %all-to-all-start.2) | async-done | bytes 1048608 | tf_op jit(solution)/shard_map/all_to_all | solution.py:43
  419.9 4.3 all-to-all-start.1
  424.2 2.3 copy.19
  426.5 5.6 %broadcast_select_fusion.1 = (bf16[1024,1280]{1,0:T(8,128)(2,1)S(1)}, bf16[1024,1280]{1,0:T(8,128)(2,1)S(1)}) fusion(bf16[1024,1280]{1,0:T(8,128)(2,1)} %collective-permute-done.25, pred[]{:T(512)S(6)} %eq.3, bf16[1024,1280]{1,0:T(8,128)(2,1)} %copy-done.2, s32[]{:T(128)S(6)} %select_n.182, bf16[1024,1280]{1,0:T(8,128)(2,1)S(1)} %constant_dynamic-update-slice_fusion), kind=kLoop, calls=%fused_computation.15 | loop fusion | flops 9175040 | bytes 13107205 | tf_op jit(solution)/shard_map/jit(_where)/select_n | solution.py:41
  432.1 4.3 fusion.7
  436.4 13.4 %all-to-all-done.1 = bf16[8,128,512]{1,2,0:T(8,128)(2,1)} async-done(((bf16[8,128,512]{1,2,0:T(8,128)(2,1)}), bf16[8,128,512]{1,2,0:T(8,128)(2,1)}, u32[]{:S(2)}, u32[]{:S(2)}) %all-to-all-start.1) | async-done | bytes 1048608 | tf_op jit(solution)/shard_map/all_to_all | solution.py:103
  449.8 1.1 constant_dynamic-slice_fusion
  450.9 1.0 copy.17
  (106 shorter events, 12.4 us)
Async XLA Ops:
  7.2 1.1 copy-start
  8.2 30.5 %copy-start.22 = (bf16[1,2048]{1,0:T(2,128)(2,1)S(1)}, bf16[1,2048]{1,0:T(2,128)(2,1)}, u32[]{:S(2)}) copy-start(bf16[1,2048]{1,0:T(2,128)(2,1)} %param.8) | copy-start | bytes 12292
  19.1 19.7 %all-to-all-start = ((bf16[64,8,512]{2,0,1:T(8,128)(2,1)}), bf16[64,8,512]{2,0,1:T(8,128)(2,1)S(1)}, u32[]{:S(2)}, u32[]{:S(2)}) async-start(bf16[64,8,512]{2,0,1:T(8,128)(2,1)} %bitcast.43), calls=%async_computation | async-start | bytes 1048576 | tf_op jit(solution)/shard_map/all_to_all | solution.py:51
  25.1 96.2 %reduce-scatter.3.cloned.1.call-start = ((), (), s32[]{:S(2)}) async-start(), calls=%async_computation.5 | async-start | bytes 2949120 | tf_op jit(solution)/shard_map/reduce_scatter | solution.py:81
  26.5 18.4 %collective-permute-start.2 = (bf16[512,1280]{1,0:T(8,128)(2,1)S(1)}, bf16[512,1280]{1,0:T(8,128)(2,1)}, u32[]{:S(2)}, u32[]{:S(2)}) collective-permute-start(bf16[512,1280]{1,0:T(8,128)(2,1)S(1)} %dynamic-slice_bitcast_fusion.1), channel_id=1, source_target_pairs={{0,16},{16,0},{1,17},{17,1},{2,18},{18,2},{3,19},{19,3},{4,20},{20... | collective-permute-start | bytes 3932168 | tf_op jit(solution)/shard_map/ppermute | solution.py:38
  38.7 5.6 %collective-permute-start = (bf16[512,512]{1,0:T(8,128)(2,1)S(1)}, bf16[512,512]{1,0:T(8,128)(2,1)S(1)}, u32[]{:S(2)}, u32[]{:S(2)}) collective-permute-start(bf16[512,512]{1,0:T(8,128)(2,1)S(1)} %bitcast.47), channel_id=1, source_target_pairs={{0,16},{16,0},{1,17},{17,1},{2,18},{18,2},{3,19},{19,3},{4,20},{20... | collective-permute-start | bytes 1572872 | tf_op jit(solution)/shard_map/ppermute | solution.py:38
  43.1 1.2 collective-permute-start.1
  44.4 2.5 copy-start.12
  44.9 1.4 copy-start.5
  50.0 137.7 %copy-start.14 = (bf16[1,2560,512]{2,1,0:T(8,128)(2,1)S(1)}, bf16[1,2560,512]{2,1,0:T(8,128)(2,1)}, u32[]{:S(2)}) copy-start(bf16[1,2560,512]{2,1,0:T(8,128)(2,1)} %param.10) | copy-start | bytes 7864324
  50.0 250.6 %reduce-scatter.5.cloned.1.call-start = ((), (), s32[]{:S(2)}) async-start(), calls=%async_computation.6 | async-start | bytes 2949120 | tf_op jit(solution)/shard_map/reduce_scatter | solution.py:81
  50.3 2.4 collective-permute-start.3
  122.6 10.9 %collective-permute-start.4 = (bf16[128,1280]{1,0:T(8,128)(2,1)S(1)}, bf16[128,1280]{1,0:T(8,128)(2,1)S(1)}, u32[]{:S(2)}, u32[]{:S(2)}) collective-permute-start(bf16[128,1280]{1,0:T(8,128)(2,1)S(1)} %fusion.32), channel_id=1, source_target_pairs={{0,2},{2,4},{4,6},{6,8},{8,10},{10,12},{12,14},{14,0},{1,3},{3,5},... | collective-permute-start | bytes 983048 | tf_op jit(solution)/shard_map/ppermute | solution.py:15
  133.4 9.9 %collective-permute-start.5 = (bf16[128,1280]{1,0:T(8,128)(2,1)S(1)}, bf16[128,1280]{1,0:T(8,128)(2,1)S(1)}, u32[]{:S(2)}, u32[]{:S(2)}) collective-permute-start(bf16[128,1280]{1,0:T(8,128)(2,1)S(1)} %collective-permute-done.4), channel_id=1, source_target_pairs={{0,2},{2,4},{4,6},{6,8},{8,10},{10,12},{12,14},{14,0},{1,3},{3,5},... | collective-permute-start | bytes 983048 | tf_op jit(solution)/shard_map/ppermute | solution.py:15
  143.4 44.3 %copy-start.17 = (bf16[128,1280]{1,0:T(8,128)(2,1)}, bf16[128,1280]{1,0:T(8,128)(2,1)S(1)}, u32[]{:S(2)}) copy-start(bf16[128,1280]{1,0:T(8,128)(2,1)S(1)} %collective-permute-done.5) | copy-start | bytes 983044
  143.4 9.8 %collective-permute-start.6 = (bf16[128,1280]{1,0:T(8,128)(2,1)S(1)}, bf16[128,1280]{1,0:T(8,128)(2,1)S(1)}, u32[]{:S(2)}, u32[]{:S(2)}) collective-permute-start(bf16[128,1280]{1,0:T(8,128)(2,1)S(1)} %collective-permute-done.5), channel_id=1, source_target_pairs={{0,2},{2,4},{4,6},{6,8},{8,10},{10,12},{12,14},{14,0},{1,3},{3,5},... | collective-permute-start | bytes 983048 | tf_op jit(solution)/shard_map/ppermute | solution.py:15
  153.2 0.7 copy-start.19
  153.9 9.8 %collective-permute-start.7 = (bf16[128,1280]{1,0:T(8,128)(2,1)S(1)}, bf16[128,1280]{1,0:T(8,128)(2,1)S(1)}, u32[]{:S(2)}, u32[]{:S(2)}) collective-permute-start(bf16[128,1280]{1,0:T(8,128)(2,1)S(1)} %collective-permute-done.6), channel_id=1, source_target_pairs={{0,2},{2,4},{4,6},{6,8},{8,10},{10,12},{12,14},{14,0},{1,3},{3,5},... | collective-permute-start | bytes 983048 | tf_op jit(solution)/shard_map/ppermute | solution.py:15
  163.7 0.7 copy-start.20
  164.4 10.4 %collective-permute-start.8 = (bf16[128,1280]{1,0:T(8,128)(2,1)S(1)}, bf16[128,1280]{1,0:T(8,128)(2,1)S(1)}, u32[]{:S(2)}, u32[]{:S(2)}) collective-permute-start(bf16[128,1280]{1,0:T(8,128)(2,1)S(1)} %collective-permute-done.7), channel_id=1, source_target_pairs={{0,2},{2,4},{4,6},{6,8},{8,10},{10,12},{12,14},{14,0},{1,3},{3,5},... | collective-permute-start | bytes 983048 | tf_op jit(solution)/shard_map/ppermute | solution.py:15
  174.8 0.7 copy-start.21
  175.6 12.1 %collective-permute-start.9 = (bf16[128,1280]{1,0:T(8,128)(2,1)S(1)}, bf16[128,1280]{1,0:T(8,128)(2,1)}, u32[]{:S(2)}, u32[]{:S(2)}) collective-permute-start(bf16[128,1280]{1,0:T(8,128)(2,1)S(1)} %collective-permute-done.8), channel_id=1, source_target_pairs={{0,2},{2,4},{4,6},{6,8},{8,10},{10,12},{12,14},{14,0},{1,3},{3,5},... | collective-permute-start | bytes 983048 | tf_op jit(solution)/shard_map/ppermute | solution.py:15
  187.7 10.1 %collective-permute-start.10 = (bf16[128,1280]{1,0:T(8,128)(2,1)}, bf16[128,1280]{1,0:T(8,128)(2,1)}, u32[]{:S(2)}, u32[]{:S(2)}) collective-permute-start(bf16[128,1280]{1,0:T(8,128)(2,1)} %collective-permute-done.9), channel_id=1, source_target_pairs={{0,2},{2,4},{4,6},{6,8},{8,10},{10,12},{12,14},{14,0},{1,3},{3,5},... | collective-permute-start | bytes 983048 | tf_op jit(solution)/shard_map/ppermute | solution.py:15
  188.8 14.0 %copy-start.7 = (bf16[128,1280]{1,0:T(8,128)(2,1)S(1)}, bf16[128,1280]{1,0:T(8,128)(2,1)}, u32[]{:S(2)}) copy-start(bf16[128,1280]{1,0:T(8,128)(2,1)} %reduce-scatter.3.cloned.1.call-done) | copy-start | bytes 983044
  188.8 14.3 %collective-permute-start.11 = (bf16[1280,512]{1,0:T(8,128)(2,1)}, bf16[1280,512]{1,0:T(8,128)(2,1)}, u32[]{:S(2)}, u32[]{:S(2)}) collective-permute-start(bf16[1280,512]{1,0:T(8,128)(2,1)} %dynamic-slice_bitcast_fusion), channel_id=1, source_target_pairs={{0,16},{16,0},{1,17},{17,1},{2,18},{18,2},{3,19},{19,3},{4,20},{20... | collective-permute-start | bytes 3932168 | tf_op jit(solution)/shard_map/ppermute | solution.py:38
  188.8 13.9 %copy-start.18 = (bf16[128,1280]{1,0:T(8,128)(2,1)S(1)}, bf16[128,1280]{1,0:T(8,128)(2,1)}, u32[]{:S(2)}) copy-start(bf16[128,1280]{1,0:T(8,128)(2,1)} %copy-done.17) | copy-start | bytes 983044
  188.8 14.3 %copy-start.15 = (bf16[1,2560,512]{2,1,0:T(8,128)(2,1)S(1)}, bf16[1,2560,512]{2,1,0:T(8,128)(2,1)}, u32[]{:S(2)}) copy-start(bf16[1,2560,512]{2,1,0:T(8,128)(2,1)} %param.10) | copy-start | bytes 7864324
  205.5 1.3 copy-start.10
  206.9 2.1 collective-permute-start.12
  207.0 17.6 %copy-start.6 = (f32[1024,512]{1,0:T(8,128)S(1)}, f32[1024,512]{1,0:T(8,128)}, u32[]{:S(2)}) copy-start(f32[1024,512]{1,0:T(8,128)} %copy-done.5) | copy-start | bytes 6291460
  210.5 17.1 %copy-start.13 = (bf16[1,512,2560]{2,1,0:T(8,128)(2,1)S(1)}, bf16[1,512,2560]{2,1,0:T(8,128)(2,1)}, u32[]{:S(2)}) copy-start(bf16[1,512,2560]{2,1,0:T(8,128)(2,1)} %param.9) | copy-start | bytes 7864324
  210.5 14.0 %collective-permute-start.13 = (bf16[512,512]{1,0:T(8,128)(2,1)S(1)}, bf16[512,512]{1,0:T(8,128)(2,1)S(1)}, u32[]{:S(2)}, u32[]{:S(2)}) collective-permute-start(bf16[512,512]{1,0:T(8,128)(2,1)S(1)} %add_convert_fusion.3), channel_id=1, source_target_pairs={{0,1},{1,0},{2,3},{3,2},{4,5},{5,4},{6,7},{7,6},{8,9},{9,8},{10,11... | collective-permute-start | bytes 1572872 | tf_op jit(solution)/shard_map/ppermute | solution.py:93
  224.8 2.0 collective-permute-start.14
  226.8 0.8 copy-start.3
  232.0 0.7 copy-start.23
  300.7 75.4 %copy-start.8 = (bf16[128,1280]{1,0:T(8,128)(2,1)S(1)}, bf16[128,1280]{1,0:T(8,128)(2,1)}, u32[]{:S(2)}) copy-start(bf16[128,1280]{1,0:T(8,128)(2,1)} %reduce-scatter.5.cloned.1.call-done) | copy-start | bytes 983044
  302.0 10.8 %collective-permute-start.15 = (bf16[128,1280]{1,0:T(8,128)(2,1)S(1)}, bf16[128,1280]{1,0:T(8,128)(2,1)S(1)}, u32[]{:S(2)}, u32[]{:S(2)}) collective-permute-start(bf16[128,1280]{1,0:T(8,128)(2,1)S(1)} %fusion.40), channel_id=1, source_target_pairs={{0,2},{2,4},{4,6},{6,8},{8,10},{10,12},{12,14},{14,0},{1,3},{3,5},... | collective-permute-start | bytes 983048 | tf_op jit(solution)/shard_map/ppermute | solution.py:15
  312.8 9.9 %collective-permute-start.16 = (bf16[128,1280]{1,0:T(8,128)(2,1)S(1)}, bf16[128,1280]{1,0:T(8,128)(2,1)S(1)}, u32[]{:S(2)}, u32[]{:S(2)}) collective-permute-start(bf16[128,1280]{1,0:T(8,128)(2,1)S(1)} %collective-permute-done.15), channel_id=1, source_target_pairs={{0,2},{2,4},{4,6},{6,8},{8,10},{10,12},{12,14},{14,0},{1,3},{3,5},... | collective-permute-start | bytes 983048 | tf_op jit(solution)/shard_map/ppermute | solution.py:15
  322.7 9.8 %collective-permute-start.17 = (bf16[128,1280]{1,0:T(8,128)(2,1)S(1)}, bf16[128,1280]{1,0:T(8,128)(2,1)S(1)}, u32[]{:S(2)}, u32[]{:S(2)}) collective-permute-start(bf16[128,1280]{1,0:T(8,128)(2,1)S(1)} %collective-permute-done.16), channel_id=1, source_target_pairs={{0,2},{2,4},{4,6},{6,8},{8,10},{10,12},{12,14},{14,0},{1,3},{3,5},... | collective-permute-start | bytes 983048 | tf_op jit(solution)/shard_map/ppermute | solution.py:15
  332.5 10.1 %collective-permute-start.18 = (bf16[128,1280]{1,0:T(8,128)(2,1)S(1)}, bf16[128,1280]{1,0:T(8,128)(2,1)S(1)}, u32[]{:S(2)}, u32[]{:S(2)}) collective-permute-start(bf16[128,1280]{1,0:T(8,128)(2,1)S(1)} %collective-permute-done.17), channel_id=1, source_target_pairs={{0,2},{2,4},{4,6},{6,8},{8,10},{10,12},{12,14},{14,0},{1,3},{3,5},... | collective-permute-start | bytes 983048 | tf_op jit(solution)/shard_map/ppermute | solution.py:15
  342.5 11.2 %collective-permute-start.19 = (bf16[128,1280]{1,0:T(8,128)(2,1)S(1)}, bf16[128,1280]{1,0:T(8,128)(2,1)S(1)}, u32[]{:S(2)}, u32[]{:S(2)}) collective-permute-start(bf16[128,1280]{1,0:T(8,128)(2,1)S(1)} %collective-permute-done.18), channel_id=1, source_target_pairs={{0,2},{2,4},{4,6},{6,8},{8,10},{10,12},{12,14},{14,0},{1,3},{3,5},... | collective-permute-start | bytes 983048 | tf_op jit(solution)/shard_map/ppermute | solution.py:15
  353.8 12.4 %collective-permute-start.20 = (bf16[128,1280]{1,0:T(8,128)(2,1)S(1)}, bf16[128,1280]{1,0:T(8,128)(2,1)S(1)}, u32[]{:S(2)}, u32[]{:S(2)}) collective-permute-start(bf16[128,1280]{1,0:T(8,128)(2,1)S(1)} %collective-permute-done.19), channel_id=1, source_target_pairs={{0,2},{2,4},{4,6},{6,8},{8,10},{10,12},{12,14},{14,0},{1,3},{3,5},... | collective-permute-start | bytes 983048 | tf_op jit(solution)/shard_map/ppermute | solution.py:15
  366.1 9.8 %collective-permute-start.21 = (bf16[128,1280]{1,0:T(8,128)(2,1)S(1)}, bf16[128,1280]{1,0:T(8,128)(2,1)S(1)}, u32[]{:S(2)}, u32[]{:S(2)}) collective-permute-start(bf16[128,1280]{1,0:T(8,128)(2,1)S(1)} %collective-permute-done.20), channel_id=1, source_target_pairs={{0,2},{2,4},{4,6},{6,8},{8,10},{10,12},{12,14},{14,0},{1,3},{3,5},... | collective-permute-start | bytes 983048 | tf_op jit(solution)/shard_map/ppermute | solution.py:15
  376.4 4.9 %copy-start.16 = (bf16[1,2560,512]{2,1,0:T(8,128)(2,1)S(1)}, bf16[1,2560,512]{2,1,0:T(8,128)(2,1)}, u32[]{:S(2)}) copy-start(bf16[1,2560,512]{2,1,0:T(8,128)(2,1)} %param.10) | copy-start | bytes 7864324
  381.3 3.8 copy-start.2
  385.2 1.5 copy-start.9
  386.7 7.1 %collective-permute-start.22 = (bf16[512,512]{1,0:T(8,128)(2,1)}, bf16[512,512]{1,0:T(8,128)(2,1)}, u32[]{:S(2)}, u32[]{:S(2)}) collective-permute-start(bf16[512,512]{1,0:T(8,128)(2,1)} %dynamic-slice_convert_fusion), channel_id=1, source_target_pairs={{0,16},{16,0},{1,17},{17,1},{2,18},{18,2},{3,19},{19,3},{4,20},{20... | collective-permute-start | bytes 1572872 | tf_op jit(solution)/shard_map/ppermute | solution.py:38
  386.7 39.8 %collective-permute-start.25 = (bf16[1024,1280]{1,0:T(8,128)(2,1)}, bf16[1024,1280]{1,0:T(8,128)(2,1)}, u32[]{:S(2)}, u32[]{:S(2)}) collective-permute-start(bf16[1024,1280]{1,0:T(8,128)(2,1)} %get-tuple-element.3), channel_id=1, source_target_pairs={{0,16},{16,0},{1,17},{17,1},{2,18},{18,2},{3,19},{19,3},{4,20},{20... | collective-permute-start | bytes 7864328 | tf_op jit(solution)/shard_map/ppermute | solution.py:38
  389.5 30.5 %all-to-all-start.2 = ((bf16[128,8,512]{0,2,1:T(8,128)(2,1)}), bf16[128,8,512]{0,2,1:T(8,128)(2,1)}, u32[]{:S(2)}, u32[]{:S(2)}) async-start(bf16[128,8,512]{0,2,1:T(8,128)(2,1)} %bitcast.45), calls=%async_computation.4 | async-start | bytes 2097152 | tf_op jit(solution)/shard_map/all_to_all | solution.py:43
  395.3 13.9 %collective-permute-start.23 = (bf16[512,512]{1,0:T(8,128)(2,1)S(1)}, bf16[512,512]{1,0:T(8,128)(2,1)S(1)}, u32[]{:S(2)}, u32[]{:S(2)}) collective-permute-start(bf16[512,512]{1,0:T(8,128)(2,1)S(1)} %add_convert_fusion.1), channel_id=1, source_target_pairs={{0,1},{1,0},{2,3},{3,2},{4,5},{5,4},{6,7},{7,6},{8,9},{9,8},{10,11... | collective-permute-start | bytes 1572872 | tf_op jit(solution)/shard_map/ppermute | solution.py:93
  398.2 13.3 %copy-start.4 = (bf16[512,512]{1,0:T(8,128)(2,1)S(1)}, bf16[512,512]{1,0:T(8,128)(2,1)}, u32[]{:S(2)}) copy-start(bf16[512,512]{1,0:T(8,128)(2,1)} %copy-done.3) | copy-start | bytes 1572868
  409.4 2.0 collective-permute-start.24
  419.9 29.8 %all-to-all-start.1 = ((bf16[8,128,512]{1,2,0:T(8,128)(2,1)}), bf16[8,128,512]{1,2,0:T(8,128)(2,1)}, u32[]{:S(2)}, u32[]{:S(2)}) async-start(bf16[8,128,512]{1,2,0:T(8,128)(2,1)} %copy.16), calls=%async_computation.3 | async-start | bytes 2097152 | tf_op jit(solution)/shard_map/all_to_all | solution.py:103
  426.5 5.6 %copy-start.11 = (bf16[8,128,512]{2,1,0:T(8,128)(2,1)S(1)}, bf16[8,128,512]{2,1,0:T(8,128)(2,1)}, u32[]{:S(2)}) copy-start(bf16[8,128,512]{2,1,0:T(8,128)(2,1)} %copy.19) | copy-start | bytes 3145732
  432.1 19.7 %copy-start.1 = (bf16[128,2048]{1,0:T(8,128)(2,1)S(1)}, bf16[128,2048]{1,0:T(8,128)(2,1)}, u32[]{:S(2)}) copy-start(bf16[128,2048]{1,0:T(8,128)(2,1)} %param.7) | copy-start | bytes 1572868
Sparse Core Ops, SparseCore 0:
  50.2 71.0 reduce-scatter.2
  232.2 68.4 reduce-scatter.4
